TPU v7x, 128 devices: a whole 4x4x4 slice. The times are simulated.
128 devices in a mesh: ao: 16 (over x, y), aux: 8 (over z, core).
Axes of the slice: x: 4, y: 4, z: 4, core: 2. Of those that a mesh axis runs over, the one named last changes fastest.
Arguments:
- blocks: bfloat16 [96, 512, 128, 128], P('ao', 'aux'), may hold values from -6 to 6
- pairs: int32 [96, 2], P('ao'), may hold values from 0 to 159, as said below
- counts: int32 [16], P('ao'), may hold values from 1 to 6, as said below
- owned_blocks: int32 [160], P('ao'), may hold values from 0 to 159, as said below
- occ_coef: bfloat16 [160, 8, 128], P('ao'), may hold values from -0.5 to 0.5
- vir_coef: bfloat16 [20480, 18432], P('ao', 'aux'), may hold values from -0.078125 to 0.078125
Outputs:
- b_tensor: bfloat16 [512, 8, 18432], P('ao', None, 'aux')
Inputs may be any that keep to these rules, and one draw needn't show every extreme that they name: `pairs`: among the used slots of one ao index, at most 3 have nu blocks whose rows one owner holds; in every draw some index reaches 3. `counts`: some ao index uses all 6 slots in every draw. `owned_blocks`: every atom block appears exactly once.
All inputs are finite; a program needn't handle non-finite values.
Results may differ from a plain program's by a relative error of at most 0.014.
Values may be sent and summed in bfloat16 or wider, within the bound.
A program may use at most 128 MiB of HBM per device.

v0:
```python
import jax
import jax.numpy as jnp
from jax import lax
from jax.sharding import PartitionSpec as P


def from_everyone(shard, axis):
    copies = jnp.broadcast_to(shard, (lax.axis_size(axis), *shard.shape))
    return lax.all_to_all(copies, axis, split_axis=0, concat_axis=0, tiled=True)


def laid_out(parts, dim):
    shape = list(parts.shape[1:])
    shape[dim] *= parts.shape[0]
    return jnp.moveaxis(parts, 0, dim).reshape(shape)


def collect(shard, axis, dim):
    parts = from_everyone(shard, axis)
    return laid_out(parts, dim)


def block_place(block_ids, owned_all):
    hits = block_ids[..., None] == owned_all
    positions = jnp.arange(owned_all.shape[0], dtype=jnp.int32)
    return jnp.sum(jnp.where(hits, positions, 0), axis=-1)


def per_device(blocks, pairs, counts, owned_blocks, occ_coef, vir_coef):
    groups = lax.axis_size("ao")
    own_index = lax.axis_index("ao")
    slot_count = blocks.shape[0]
    aux_depth = blocks.shape[1]
    block_width = blocks.shape[3]
    occupied = occ_coef.shape[1]
    all_pairs, all_counts, all_owned = (
        lax.all_gather(pairs, "ao", axis=0, tiled=True),
        lax.all_gather(counts, "ao", axis=0, tiled=True),
        lax.all_gather(owned_blocks, "ao", axis=0, tiled=True),
    )
    occ_all = collect(occ_coef, "ao", 0)
    total_blocks = all_owned.shape[0]
    per_owner = total_blocks // groups
    slot_ids = jnp.arange(slot_count, dtype=jnp.int32)
    in_use = slot_ids < counts[0]
    occ_pick = occ_all[block_place(pairs[:, 0], all_owned)]
    slab_values = jnp.einsum("sim,spmn->spin", occ_pick, blocks, preferred_element_type=jnp.float32)
    slab_values = jnp.where(in_use[:, None, None, None], slab_values, 0.0).astype(jnp.bfloat16)
    flat_slabs = slab_values.reshape(slot_count, aux_depth * occupied, block_width)
    place_all = block_place(all_pairs[:, 1], all_owned).reshape(groups, slot_count)
    owner_all = place_all // per_owner
    local_all = place_all % per_owner
    live_all = slot_ids[None, :] < all_counts[:, None]
    mine_all = live_all & (owner_all == own_index)
    local_ids = jnp.arange(per_owner, dtype=jnp.int32)
    slabs_got = lax.all_gather(flat_slabs, "ao", axis=0, tiled=True)
    assign = (
        mine_all.reshape(-1)[None, :] & (local_all.reshape(-1)[None, :] == local_ids[:, None])
    ).astype(jnp.bfloat16)
    summed = jnp.einsum("lt,tqm->qlm", assign, slabs_got, preferred_element_type=jnp.float32)
    rows_local = summed.reshape(summed.shape[0], per_owner * block_width).astype(jnp.bfloat16)
    rows_whole = lax.all_gather(rows_local, "aux", axis=0, tiled=True)
    share = rows_whole.shape[0] // groups
    result = lax.psum_scatter(
        jnp.dot(rows_whole, vir_coef, preferred_element_type=jnp.float32).astype(jnp.bfloat16),
        "ao",
        scatter_dimension=0,
        tiled=True,
    ).astype(jnp.float32)
    return result.reshape(share // occupied, occupied, vir_coef.shape[1]).astype(jnp.bfloat16)


def solution(mesh):
    in_specs = (
        P("ao", "aux", None, None),
        P("ao", None),
        P("ao"),
        P("ao"),
        P("ao", None, None),
        P("ao", "aux"),
    )
    out_specs = P("ao", None, "aux")
    return jax.shard_map(
        per_device, mesh=mesh, in_specs=in_specs, out_specs=out_specs, check_vma=False
    )
```

profile of v0, /device:TPU:0, one launch (start us, length us, event | category | flops | bytes accessed | tf_op | source)
XLA Modules:
  0.0 364.3 jit_solution(770621144552346490)
XLA Ops:
  6.5 0.0 copy-start
  6.5 1.5 broadcast_in_dim.39
  8.0 7.1 %all-to-all-start = ((bf16[16,10,8,128]{3,2,1,0:T(8,128)(2,1)}), bf16[16,10,8,128]{3,2,1,0:T(8,128)(2,1)S(1)}, u32[]{:S(2)}, u32[]{:S(2)}) async-start(bf16[16,10,8,128]{3,2,1,0:T(8,128)(2,1)} %broadcast_in_dim.39), calls=%async_computation | async-start | bytes 655360 | tf_op jit(solution)/shard_map/all_to_all | solution.py:9
  15.2 0.0 all-gather.4.cloned.1.call-start
  15.9 0.7 slice_bitcast_fusion.1
  16.6 1.3 dynamic-slice
  18.5 0.7 dynamic-update-slice.1
  19.3 0.8 dynamic-update-slice
  20.1 16.6 %all-reduce.2 = (s32[160]{0:T(256)S(1)}, s32[16]{0:T(128)S(1)}) all-reduce(s32[160]{0:T(256)S(1)} %dynamic-update-slice, s32[16]{0:T(128)S(1)} %dynamic-update-slice.1), channel_id=1, replica_groups=mesh['ao'=16,'aux'=8] {'ao'}, use_global_device_ids=true, to_apply=%add | all-reduce | flops 176 | bytes 1408
  36.7 0.2 select_reduce_fusion.1
  36.9 0.0 all-to-all-done
  36.9 0.6 gather_fusion
  37.5 7.2 %fusion.4 = bf16[6,512,128]{2,1,0:T(8,128)(2,1)} fusion(bf16[6,64,128,128]{3,2,1,0:T(8,128)(2,1)} %param.6, pred[6]{0:T(512)(128)(4,1)S(1)} %iota_compare_fusion.2, bf16[6,8,128]{2,1,0:T(8,128)(2,1)S(1)} %gather_fusion), kind=kOutput, calls=%fused_computation.6 | convolution fusion | flops 101449728 | bytes 13381638 | tf_op jit(solution)/shard_map/sim,spmn->spin/dot_general | solution.py:47
  44.7 0.0 all-gather.4.cloned.1.call-update
  44.7 0.0 all-gather.6.cloned.1.call-start
  44.8 0.1 iota_compare_fusion.1
  44.9 0.1 lt.52
  45.0 0.0 copy-done
  45.0 21.7 %all-gather = s32[16,6,2]{1,2,0:T(2,128)S(1)} all-gather(s32[1,6,2]{1,2,0:T(2,128)S(1)} %bitcast.37), channel_id=1, replica_groups=mesh['ao'=16,'aux'=8] {'ao'}, dimensions={0}, use_global_device_ids=true | all-gather | bytes 816 | tf_op jit(solution)/shard_map/all_gather | solution.py:37
  66.6 0.1 reshape.79
  66.7 0.1 select_reduce_fusion
  66.9 65.8 %all-gather.4.cloned.1.call-done = bf16[96,512,128]{2,1,0:T(8,128)(2,1)} async-done(((bf16[6,512,128]{2,1,0:T(8,128)(2,1)}), bf16[96,512,128]{2,1,0:T(8,128)(2,1)}) %all-gather.4.cloned.1.call-update) | async-done | bytes 12582928 | tf_op jit(solution)/shard_map/all_gather | solution.py:56
  132.7 11.5 %convert_bitcast_fusion = bf16[512,10,128]{2,1,0:T(8,128)(2,1)S(1)} fusion(bf16[96,512,128]{2,1,0:T(8,128)(2,1)} %all-gather.4.cloned.1.call-done, s32[96]{0:T(128)S(1)} %and_select_fusion, pred[96]{0:T(512)(128)(4,1)S(1)} %compare_and_fusion), kind=kOutput, calls=%fused_computation.4 | convolution fusion | flops 126486400 | bytes 13894112 | tf_op jit(solution)/shard_map/lt,tqm->qlm/dot_general | solution.py:60
  144.2 2.6 copy.16
  146.8 0.0 all-gather.6.cloned.1.call-update
  146.8 0.2 reduce-scatter.2.cloned.1.call-start
  147.0 58.3 %all-gather.6.cloned.1.call-done = bf16[4096,1280]{0,1:T(8,128)(2,1)} async-done(((bf16[512,1280]{0,1:T(8,128)(2,1)}), bf16[4096,1280]{0,1:T(8,128)(2,1)}) %all-gather.6.cloned.1.call-update) | async-done | bytes 10485776 | tf_op jit(solution)/shard_map/all_gather | solution.py:62
  205.3 31.2 %convolution_convert_fusion = bf16[4096,2304]{1,0:T(8,128)(2,1)} fusion(bf16[4096,1280]{0,1:T(8,128)(2,1)} %all-gather.6.cloned.1.call-done, bf16[1280,2304]{1,0:T(8,128)(2,1)} %param.11), kind=kOutput, calls=%fused_computation.1 | convolution fusion | flops 24168628224 | bytes 35258368 | tf_op jit(solution)/shard_map/dot_general | solution.py:65
  236.5 0.0 reduce-scatter.2.cloned.1.call-update
  236.5 121.2 %reduce-scatter.2.cloned.1.call-done = bf16[256,2304]{1,0:T(8,128)(2,1)} async-done(((bf16[4096,2304]{1,0:T(8,128)(2,1)}), bf16[256,2304]{1,0:T(8,128)(2,1)}) %reduce-scatter.2.cloned.1.call-update) | async-done | bytes 1179664 | tf_op jit(solution)/shard_map/reduce_scatter | solution.py:64
  (9 shorter events, 0.1 us)
Async XLA Ops:
  6.5 38.4 %copy-start = (s32[6,2]{0,1:T(2,128)S(1)}, s32[6,2]{0,1:T(2,128)}, u32[]{:S(2)}) copy-start(s32[6,2]{0,1:T(2,128)} %param.7) | copy-start | bytes 148
  8.0 28.9 %all-to-all-start = ((bf16[16,10,8,128]{3,2,1,0:T(8,128)(2,1)}), bf16[16,10,8,128]{3,2,1,0:T(8,128)(2,1)S(1)}, u32[]{:S(2)}, u32[]{:S(2)}) async-start(bf16[16,10,8,128]{3,2,1,0:T(8,128)(2,1)} %broadcast_in_dim.39), calls=%async_computation | async-start | bytes 655360 | tf_op jit(solution)/shard_map/all_to_all | solution.py:9
  15.2 117.5 %all-gather.4.cloned.1.call-start = ((), (), s32[]{:S(2)}) async-start(), calls=%async_computation.2 | async-start | bytes 13369344 | tf_op jit(solution)/shard_map/all_gather | solution.py:56
  44.7 160.6 %all-gather.6.cloned.1.call-start = ((), (), s32[]{:S(2)}) async-start(), calls=%async_computation.3 | async-start | bytes 11796480 | tf_op jit(solution)/shard_map/all_gather | solution.py:62
  146.8 211.0 %reduce-scatter.2.cloned.1.call-start = ((), (), s32[]{:S(2)}) async-start(), calls=%async_computation.4 | async-start | bytes 20054016 | tf_op jit(solution)/shard_map/reduce_scatter | solution.py:64
Sparse Core Ops, SparseCore 0:
  44.9 87.8 all-gather.3
  146.9 58.3 all-gather.5
  236.7 121.0 reduce-scatter.1
where the time goes:
time: 365 us; the launch traced here: 364 us
  waiting for transfers between devices  245 us (67%)
  matrix products  49.9 us (14%)
  blocking collectives  38.3 us (10%)
  between operations  14.5 us (4%)
  local copies, waits for them, and re-layouts  8.39 us (2%)
  starting transfers between devices  7.45 us (2%)
    reduce_scatter x1, waiting for transfers between devices, per_device(): lax.psum_scatter(jnp.dot(rows_whole, vir_coef, preferred_element_type=jnp...  121 us
    all_gather x1, waiting for transfers between devices, per_device(): slabs_got = lax.all_gather(flat_slabs, 'ao', axis=0, tiled=True)  65.8 us
    all_gather x1, waiting for transfers between devices, per_device(): rows_whole = lax.all_gather(rows_local, 'aux', axis=0, tiled=True)  58.3 us
    dot_general x1, matrix products, per_device(): jnp.dot(rows_whole, vir_coef, preferred_element_type=jnp.float32)  31.2 us
    all_gather x1, blocking collectives, per_device(): lax.all_gather(pairs, 'ao', axis=0, tiled=True)  21.7 us
    unnamed x1, blocking collectives  16.6 us
    dot_general x1, matrix products, per_device(): jnp.einsum('lt,tqm->qlm', assign, slabs_got, preferred_element_type=jnp.f...  11.5 us
  transfers between devices with their start and end apart: 4, of which 3 were waited for; matrix products, arithmetic and copies ran while one was open for 1% of the time, Pallas kernels for 0%

commit v1 on v0

v1 whole, which is shorter than its diff:
```python
import functools

import jax
import jax.numpy as jnp
from jax import lax
from jax.experimental import pallas as pl
from jax.experimental.pallas import tpu as pltpu
from jax.sharding import PartitionSpec as P

MESH = pl.DeviceIdType.MESH
VMEM = pltpu.VMEM
DMA = pltpu.SemaphoreType.DMA


def greet(peers):
    barrier = pltpu.get_barrier_semaphore()
    for peer in peers:
        pl.semaphore_signal(barrier, inc=1, device_id=peer, device_id_type=MESH)
    pl.semaphore_wait(barrier, len(peers))


def remote(src, dst, send_sem, recv_sem, peer):
    return pltpu.make_async_remote_copy(
        src_ref=src, dst_ref=dst, send_sem=send_sem, recv_sem=recv_sem,
        device_id=peer, device_id_type=MESH,
    )


def tables_kernel(groups, ints_ref, occ_ref, ints_all, occ_all, send, recv):
    me = lax.axis_index("ao")
    peers = [{"ao": lax.rem(me + k, groups)} for k in range(1, groups)]
    greet(peers)
    copies = []
    for k, peer in enumerate(peers):
        copies.append(remote(ints_ref, ints_all.at[me], send.at[0, k], recv.at[0, k], peer))
        copies.append(remote(occ_ref, occ_all.at[me], send.at[1, k], recv.at[1, k], peer))
    for copy in copies:
        copy.start()
    ints_all[me] = ints_ref[...]
    occ_all[me] = occ_ref[...]
    for copy in copies:
        copy.wait()


def regroup_kernel(groups, per_owner, half_ref, pick_ref, out_ref, got, parts, send, recv):
    me = lax.axis_index("ao")
    peers = [{"ao": lax.rem(me + k, groups)} for k in range(1, groups)]
    rows = half_ref.shape[2]
    mine = pl.ds(pl.multiple_of(me * rows, 16), rows)
    greet(peers)
    copies = []
    for k, peer in enumerate(peers):
        copies.append(
            remote(half_ref.at[peer["ao"]], got.at[:, mine, :], send.at[0, k], recv.at[0, k], peer)
        )
    for copy in copies:
        copy.start()
    got[:, mine, :] = half_ref[me]
    for copy in copies:
        copy.wait_recv()
    owner_rows = per_owner * 8
    slot = lax.rem(me, 8) * 2 + me // 8

    def summed(owner, dst):
        pick = pick_ref[pl.ds(pl.multiple_of(owner * owner_rows, 16), owner_rows), :]
        for u in range(2):
            both = jnp.concatenate([got[2 * u], got[2 * u + 1]], axis=1)
            total = jnp.dot(pick, both, preferred_element_type=jnp.float32)
            for l in range(per_owner):
                tile = jnp.concatenate(
                    [total[8 * l:8 * l + 8, :128], total[8 * l:8 * l + 8, 128:]], axis=0
                )
                dst[16 * u:16 * u + 16, 128 * l:128 * l + 128] = tile.astype(jnp.bfloat16)

    def handed(k):
        owner = lax.rem(me + k, groups)
        return remote(parts.at[owner], out_ref.at[slot], send.at[1, k - 1], recv.at[1, k - 1], {"ao": owner})

    def step(k, carry):
        owner = lax.rem(me + k, groups)
        summed(owner, parts.at[owner])

        @pl.when(k > 1)
        def _():
            handed(k - 1).start()

        return carry

    lax.fori_loop(1, groups, step, 0)
    summed(me, out_ref.at[slot])
    handed(groups - 1).start()
    for copy in copies:
        copy.wait_send()

    def finish(k, carry):
        handed(k).wait()
        return carry

    lax.fori_loop(1, groups, finish, 0)


def product_kernel(
    chunks, left_ref, vir_hbm, out_ref, vir, left, part,
    got1, got2, got3, got4, vir_sem,
    c_send, c_recv, s1_send, s1_recv, s2_send, s2_recv, s3_send, s3_recv, s4_send, s4_recv,
):
    ao, aux = lax.axis_index("ao"), lax.axis_index("aux")
    x, y = ao // 4, lax.rem(ao, 4)
    z, core = aux // 2, lax.rem(aux, 2)

    def turn(v, by):
        return lax.rem(v + by + 4, 4)

    def at_xy(xx, yy):
        return {"ao": xx * 4 + yy}

    def at_z(zz, cc):
        return {"aux": zz * 2 + cc}

    up, down, other = at_z(turn(z, 1), core), at_z(turn(z, -1), core), at_z(z, 1 - core)
    near = [
        [[at_xy(turn(x, 1), y), at_xy(turn(x, -1), y)], [at_xy(x, turn(y, 1)), at_xy(x, turn(y, -1))]],
        [[at_xy(x, turn(y, 1)), at_xy(x, turn(y, -1))], [at_xy(turn(x, 1), y), at_xy(turn(x, -1), y)]],
    ]
    major, minor = [x, y], [y, x]
    sides = (1, -1)
    load = pltpu.make_async_copy(vir_hbm, vir, vir_sem)
    load.start()
    greet([up, down, other] + near[0][0] + near[0][1])

    unit = left_ref.shape[1]
    mid = unit // 2

    def rows_of(index, start=0, size=unit):
        return pl.ds(pl.multiple_of(index * unit + start, 16), size)

    def left_copy(q, k, src, rows, peer):
        return remote(src, left.at[q, rows], c_send.at[k, q], c_recv.at[k, q], peer)

    def index_of(zz, cc):
        return zz * 2 + cc

    def own_copy(q, k):
        peer = (up, down, other)[k]
        return left_copy(q, k, left_ref.at[q], rows_of(aux), peer)

    def half_copy(q, k):
        zz = turn(z, -1) if k == 0 else turn(z, 1)
        rows = rows_of(index_of(zz, core), mid * k, mid)
        return left_copy(q, 3 + k, left.at[q, rows], rows, (up, down)[k])

    def side_copy(q, k):
        zz = turn(z, (-1, 1, 2)[k])
        rows = rows_of(index_of(zz, core))
        return left_copy(q, 5 + k, left.at[q, rows], rows, other)

    def gather_start(q):
        for k in range(3):
            own_copy(q, k).start()
        left[q, rows_of(aux)] = left_ref[q]

    def gather_near(q):
        for k in range(2):
            own_copy(q, k).wait_recv()
            half_copy(q, k).start()
            side_copy(q, k).start()

    def gather_far(q):
        for k in range(2):
            half_copy(q, k).wait_recv()
        side_copy(q, 2).start()

    def gather_wait(q):
        own_copy(q, 2).wait_recv()
        for k in range(3):
            side_copy(q, k).wait_recv()

    def multiply(q):
        def tile(n, carry):
            cols = pl.ds(pl.multiple_of(n * 256, 256), 256)
            term = jnp.dot(left[q], vir[:, cols], preferred_element_type=jnp.float32)
            part[q, :, :, :, :, cols] = term.astype(jnp.bfloat16).reshape(4, 4, 2, 16, 256)
            return carry

        lax.fori_loop(0, vir.shape[1] // 256, tile, 0)

    def slab(q, f, a, b):
        return part.at[q, a, b, 0] if f == 0 else part.at[q, b, a, 1]

    half_cols = vir.shape[1] // 2

    def copy1(q, f, d):
        return remote(
            slab(q, f, turn(major[f], 2), pl.ds(2 * d, 2)), got1.at[f, d, q],
            s1_send.at[f, d, q], s1_recv.at[f, d, q], near[f][0][d],
        )

    def copy2(q, f, d):
        return remote(
            slab(q, f, turn(major[f], sides[d]), pl.ds(0, 4)), got2.at[f, d, q],
            s2_send.at[f, d, q], s2_recv.at[f, d, q], near[f][0][d],
        )

    def copy3(q, f, d):
        return remote(
            slab(q, f, major[f], turn(minor[f], 2)).at[:, pl.ds(d * half_cols, half_cols)], got3.at[f, d, q],
            s3_send.at[f, d, q], s3_recv.at[f, d, q], near[f][1][d],
        )

    def copy4(q, f, d):
        return remote(
            slab(q, f, major[f], turn(minor[f], sides[d])), got4.at[f, d, q],
            s4_send.at[f, d, q], s4_recv.at[f, d, q], near[f][1][d],
        )

    pairs = [(f, d) for f in range(2) for d in range(2)]

    def wide(v):
        return v.astype(jnp.float32)

    def stage1(q):
        for f, d in pairs:
            copy1(q, f, d).start()

    def stage2(q):
        for f, d in pairs:
            copy1(q, f, d).wait_recv()
            mine = slab(q, f, turn(major[f], sides[d]), pl.ds(2 * d, 2))
            mine[...] = (wide(mine[...]) + wide(got1[f, d, q])).astype(jnp.bfloat16)
            copy2(q, f, d).start()

    def stage3(q):
        for f in range(2):
            for d in range(2):
                copy2(q, f, d).wait_recv()
            for j in (2, 1, 3, 0):
                b = turn(minor[f], j)
                mine = slab(q, f, major[f], b)
                mine[...] = (
                    wide(mine[...]) + wide(got2[f, 0, q, b]) + wide(got2[f, 1, q, b])
                ).astype(jnp.bfloat16)
            for d in range(2):
                copy3(q, f, d).start()

    def stage4(q):
        for f, d in pairs:
            copy3(q, f, d).wait_recv()
            mine = slab(q, f, major[f], turn(minor[f], sides[d])).at[:, pl.ds(d * half_cols, half_cols)]
            mine[...] = (wide(mine[...]) + wide(got3[f, d, q])).astype(jnp.bfloat16)
            copy4(q, f, d).start()

    def stage5(q):
        for f in range(2):
            for d in range(2):
                copy4(q, f, d).wait_recv()
            mine = slab(q, f, major[f], minor[f])
            out_ref[pl.ds(pl.multiple_of(q * 32 + f * 16, 16), 16), :] = (
                wide(mine[...]) + wide(got4[f, 0, q]) + wide(got4[f, 1, q])
            ).astype(jnp.bfloat16)

    gather_start(0)
    gather_start(1)
    gather_near(0)
    gather_start(2)
    gather_near(1)
    gather_far(0)
    load.wait()

    def step(it, carry):
        def on(q, work):
            @pl.when(jnp.logical_and(q >= 0, q < chunks))
            def _():
                work(q)

        on(it, gather_wait)
        on(it, multiply)
        on(it, stage1)
        on(it + 3, gather_start)
        on(it + 2, gather_near)
        on(it - 1, stage2)
        on(it + 1, gather_far)
        on(it - 2, stage3)
        on(it - 3, stage4)
        on(it - 4, stage5)
        return carry

    lax.fori_loop(0, chunks + 4, step, 0)

    def finish(q, carry):
        for k in range(3):
            own_copy(q, k).wait_send()
            side_copy(q, k).wait_send()
        for k in range(2):
            half_copy(q, k).wait_send()
        for f, d in pairs:
            copy1(q, f, d).wait_send()
            copy2(q, f, d).wait_send()
            copy3(q, f, d).wait_send()
            copy4(q, f, d).wait_send()
        return carry

    lax.fori_loop(0, chunks, finish, 0)


def params(collective_id, vmem=None):
    return pltpu.CompilerParams(
        collective_id=collective_id, has_side_effects=True, vmem_limit_bytes=vmem
    )


def block_place(block_ids, owned_all):
    hits = block_ids[..., None] == owned_all
    positions = jnp.arange(owned_all.shape[0], dtype=jnp.int32)
    return jnp.sum(jnp.where(hits, positions, 0), axis=-1)


def per_device(blocks, pairs, counts, owned_blocks, occ_coef, vir_coef):
    groups = lax.axis_size("ao")
    slots, depth, _, width = blocks.shape
    occupied = occ_coef.shape[1]
    per_owner = owned_blocks.shape[0]
    cols = vir_coef.shape[1]
    bf16, i32 = jnp.bfloat16, jnp.int32
    spec = pl.BlockSpec(memory_space=VMEM)

    n_ints = per_owner + 2 * slots + 1
    ints = jnp.concatenate([owned_blocks, pairs[:, 0], pairs[:, 1], counts])
    ints = jnp.pad(ints[None, :], ((0, 7), (0, 128 - n_ints)))
    ints_all, occ_all = pl.pallas_call(
        functools.partial(tables_kernel, groups),
        out_shape=(
            jax.ShapeDtypeStruct((groups, 8, 128), i32),
            jax.ShapeDtypeStruct((groups, per_owner * occupied, width), bf16),
        ),
        in_specs=[spec] * 2,
        out_specs=(spec, spec),
        scratch_shapes=[DMA((2, groups - 1)), DMA((2, groups - 1))],
        compiler_params=params(0),
    )(ints, occ_coef.reshape(per_owner * occupied, width))

    ints_all = ints_all[:, 0, :n_ints]
    owned_all = ints_all[:, :per_owner].reshape(-1)
    second_all = ints_all[:, per_owner + slots:per_owner + 2 * slots]
    live = jnp.arange(slots, dtype=i32)[None, :] < ints_all[:, n_ints - 1:]
    second_all = jnp.where(live, second_all, -1).reshape(-1)
    orbital = jnp.arange(occupied, dtype=i32)
    rows = (owned_all[:, None] * occupied + orbital).reshape(-1)
    hits = (jnp.where(second_all < 0, -occupied, second_all * occupied)[:, None] + orbital).reshape(-1)
    pick = (rows[:, None] == hits[None, :]).astype(bf16)

    occ_all = occ_all.reshape(groups * per_owner, occupied, width)
    occ_pick = occ_all[block_place(pairs[:, 0], owned_all)]
    half = jnp.einsum("sim,spmn->psin", occ_pick, blocks, preferred_element_type=jnp.float32)
    in_use = jnp.arange(slots, dtype=i32) < counts[0]
    half = jnp.where(in_use[None, :, None, None], half, 0.0).astype(bf16)
    half = half.reshape(groups, depth // groups, slots * occupied, width)

    piece = depth // groups * occupied
    left = pl.pallas_call(
        functools.partial(regroup_kernel, groups, per_owner),
        out_shape=jax.ShapeDtypeStruct((groups, piece, per_owner * width), bf16),
        in_specs=[spec] * 2,
        out_specs=spec,
        scratch_shapes=[
            VMEM((depth // groups, groups * slots * occupied, width), bf16),
            VMEM((groups, piece, per_owner * width), bf16),
            DMA((2, groups - 1)),
            DMA((2, groups - 1)),
        ],
        compiler_params=params(1),
    )(half, pick)

    chunks = 8
    left = left.reshape(chunks, 2 * piece, per_owner * width)
    sems = [DMA((8, chunks)), DMA((8, chunks))] + [DMA((2, 2, chunks))] * 8
    out = pl.pallas_call(
        functools.partial(product_kernel, chunks),
        out_shape=jax.ShapeDtypeStruct((groups * 16, cols), bf16),
        in_specs=[spec, pl.BlockSpec(memory_space=pl.ANY)],
        out_specs=spec,
        scratch_shapes=[
            VMEM(vir_coef.shape, bf16),
            VMEM((chunks, 8 * 2 * piece, per_owner * width), bf16),
            VMEM((chunks, 4, 4, 2, 16, cols), bf16),
            VMEM((2, 2, chunks, 2, 16, cols), bf16),
            VMEM((2, 2, chunks, 4, 16, cols), bf16),
            VMEM((2, 2, chunks, 16, cols // 2), bf16),
            VMEM((2, 2, chunks, 16, cols), bf16),
            DMA,
        ] + sems,
        compiler_params=params(2, 66 * 1024 * 1024 - 3 * 1024 * 1024),
    )(left, vir_coef)
    return out.reshape(-1, occupied, cols)


def solution(mesh):
    in_specs = (
        P("ao", "aux", None, None),
        P("ao", None),
        P("ao"),
        P("ao"),
        P("ao", None, None),
        P("ao", "aux"),
    )
    out_specs = P("ao", None, "aux")
    return jax.shard_map(
        per_device, mesh=mesh, in_specs=in_specs, out_specs=out_specs, check_vma=False
    )
```

time: 365 us -> 201 us (0.55)
  waiting for transfers between devices: 245 us -> 0 us
  Pallas kernels: 0 us -> 183 us
  matrix products: 49.9 us -> 6.31 us
  blocking collectives: 38.3 us -> 0 us
  between operations: 14.5 us -> 0.75 us
  starting transfers between devices: 7.45 us -> 0 us
    pallas_call x0 -> x3, Pallas kernels: none -> 183 us  [the longest x1 133 us: per_device(): pl.pallas_call(functools.partial(product_kernel, chunks), out_shape=jax.S...]
    all_gather x2 -> x0, waiting for transfers between devices: 124 us -> none  [the longest x1 65.8 us: per_device(): slabs_got = lax.all_gather(flat_slabs, 'ao', axis=0, tiled=True)]
    reduce_scatter x1 -> x0, waiting for transfers between devices: 121 us -> none  [per_device(): lax.psum_scatter(jnp.dot(rows_whole, vir_coef, preferred_element_type=jnp...]
    dot_general x3 -> x1, matrix products: 49.9 us -> 6.31 us  [per_device(): jnp.einsum('sim,spmn->psin', occ_pick, blocks, preferred_element_type=jnp...]
    all_gather x1 -> x0, blocking collectives: 21.7 us -> none  [per_device(): lax.all_gather(pairs, 'ao', axis=0, tiled=True)]
    unnamed x1 -> x0, blocking collectives: 16.6 us -> none
    all_to_all x1 -> x0, starting transfers between devices: 7.15 us -> none  [from_everyone(): return lax.all_to_all(copies, axis, split_axis=0, concat_axis=0, tiled=True)]
  transfers between devices with their start and end apart: 4 -> 0, of which waited for: 3 -> 0; matrix products, arithmetic and copies ran while one was open for 1% -> 0% of each run, Pallas kernels for 0% -> 0%
where the time goes in v1:
time: 201 us; the launch traced here: 200 us
  Pallas kernels  183 us (91%)
  local copies, waits for them, and re-layouts  7.67 us (4%)
  matrix products  6.31 us (3%)
  other arithmetic  2.83 us (1%)
    pallas_call x1, Pallas kernels, per_device(): pl.pallas_call(functools.partial(product_kernel, chunks), out_shape=jax.S...  133 us
    pallas_call x1, Pallas kernels, per_device(): pl.pallas_call(functools.partial(regroup_kernel, groups, per_owner), out_...  36.6 us
    pallas_call x1, Pallas kernels, per_device(): pl.pallas_call(functools.partial(tables_kernel, groups), out_shape=(jax.S...  13.8 us
    dot_general x1, matrix products, per_device(): jnp.einsum('sim,spmn->psin', occ_pick, blocks, preferred_element_type=jnp...  6.31 us

profile of v1, /device:TPU:0, one launch (start us, length us, event | category | flops | bytes accessed | tf_op | source)
XLA Modules:
  0.0 200.5 jit_solution(2590535547002229910)
XLA Ops:
  0.7 0.8 slice_bitcast_fusion.1
  1.4 0.7 add_bitcast_fusion
  2.2 0.6 pad.4.ints_ref
  2.8 13.8 %shard_map.64 = (s32[16,8,128]{2,1,0:T(8,128)}, bf16[16,80,128]{2,1,0:T(8,128)(2,1)}) custom-call(s32[8,128]{1,0:T(8,128)} %pad.4.ints_ref, bf16[80,128]{1,0:T(8,128)(2,1)} %bitcast.33), custom_call_target="tpu_custom_call" | custom-call | tf_op jit(solution)/shard_map/pallas_call | solution.py:329
  16.6 0.8 slice.21
  17.4 0.2 slice_reduce_fusion
  17.6 0.1 eq.29
  17.7 0.2 select_reduce_fusion
  17.9 1.5 gather_fusion
  19.5 0.1 multiply_select_fusion
  19.5 0.1 select_n.39
  19.6 0.1 iota_add_fusion.1
  19.7 0.1 add.60
  19.8 0.1 iota_add_fusion
  19.9 0.1 add.56
  20.0 6.3 %fusion = bf16[64,6,8,128]{3,2,0,1:T(8,128)(2,1)S(1)} fusion(bf16[6,64,128,128]{3,2,1,0:T(8,128)(2,1)} %param.6, pred[6]{0:T(512)(128)(4,1)S(1)} %iota_compare_fusion.1, bf16[6,8,128]{2,1,0:T(8,128)(2,1)S(1)} %gather_fusion), kind=kOutput, calls=%fused_computation.3 | convolution fusion | flops 101449728 | bytes 13381638 | tf_op jit(solution)/shard_map/sim,spmn->psin/dot_general | solution.py:353
  26.3 1.0 copy.9
  27.3 1.7 compare_convert_fusion.pick_ref
  29.0 36.6 %shard_map.65 = bf16[16,32,1280]{2,1,0:T(8,128)(2,1)} custom-call(bf16[16,4,48,128]{3,2,1,0:T(8,128)(2,1)} %bitcast.29, bf16[1280,768]{1,0:T(8,128)(2,1)} %compare_convert_fusion.pick_ref), custom_call_target="tpu_custom_call" | custom-call | tf_op jit(solution)/shard_map/pallas_call | solution.py:359
  65.6 132.5 %shard_map.66 = bf16[256,2304]{1,0:T(8,128)(2,1)} custom-call(bf16[8,64,1280]{2,1,0:T(8,128)(2,1)} %bitcast.27, bf16[1280,2304]{1,0:T(8,128)(2,1)} %vir_hbm.1), custom_call_target="tpu_custom_call" | custom-call | tf_op jit(solution)/shard_map/pallas_call | solution.py:376
  198.1 2.4 %copy.13 = bf16[32,8,2304]{2,1,0:T(8,128)(2,1)} copy(bf16[32,8,2304]{2,1,0:T(8,128)(2,1)} %bitcast.28) | data formatting | bytes 2359296
  (4 shorter events, 0.0 us)

commit v2 on v1

--- a/solution.py
+++ b/solution.py
@@ -42,66 +42,9 @@
         copy.wait()
 
 
-def regroup_kernel(groups, per_owner, half_ref, pick_ref, out_ref, got, parts, send, recv):
-    me = lax.axis_index("ao")
-    peers = [{"ao": lax.rem(me + k, groups)} for k in range(1, groups)]
-    rows = half_ref.shape[2]
-    mine = pl.ds(pl.multiple_of(me * rows, 16), rows)
-    greet(peers)
-    copies = []
-    for k, peer in enumerate(peers):
-        copies.append(
-            remote(half_ref.at[peer["ao"]], got.at[:, mine, :], send.at[0, k], recv.at[0, k], peer)
-        )
-    for copy in copies:
-        copy.start()
-    got[:, mine, :] = half_ref[me]
-    for copy in copies:
-        copy.wait_recv()
-    owner_rows = per_owner * 8
-    slot = lax.rem(me, 8) * 2 + me // 8
-
-    def summed(owner, dst):
-        pick = pick_ref[pl.ds(pl.multiple_of(owner * owner_rows, 16), owner_rows), :]
-        for u in range(2):
-            both = jnp.concatenate([got[2 * u], got[2 * u + 1]], axis=1)
-            total = jnp.dot(pick, both, preferred_element_type=jnp.float32)
-            for l in range(per_owner):
-                tile = jnp.concatenate(
-                    [total[8 * l:8 * l + 8, :128], total[8 * l:8 * l + 8, 128:]], axis=0
-                )
-                dst[16 * u:16 * u + 16, 128 * l:128 * l + 128] = tile.astype(jnp.bfloat16)
-
-    def handed(k):
-        owner = lax.rem(me + k, groups)
-        return remote(parts.at[owner], out_ref.at[slot], send.at[1, k - 1], recv.at[1, k - 1], {"ao": owner})
-
-    def step(k, carry):
-        owner = lax.rem(me + k, groups)
-        summed(owner, parts.at[owner])
-
-        @pl.when(k > 1)
-        def _():
-            handed(k - 1).start()
-
-        return carry
-
-    lax.fori_loop(1, groups, step, 0)
-    summed(me, out_ref.at[slot])
-    handed(groups - 1).start()
-    for copy in copies:
-        copy.wait_send()
-
-    def finish(k, carry):
-        handed(k).wait()
-        return carry
-
-    lax.fori_loop(1, groups, finish, 0)
-
-
 def product_kernel(
-    chunks, left_ref, vir_hbm, out_ref, vir, left, part,
-    got1, got2, got3, got4, vir_sem,
+    groups, chunks, depth, half_ref, pick_ref, vir_hbm, out_ref, got, parts, owned, vir, left, part,
+    got1, got2, got3, got4, vir_sem, p1_send, p1_recv, p2_send, p2_recv,
     c_send, c_recv, s1_send, s1_recv, s2_send, s2_recv, s3_send, s3_recv, s4_send, s4_recv,
 ):
     ao, aux = lax.axis_index("ao"), lax.axis_index("aux")
@@ -126,9 +69,71 @@
     sides = (1, -1)
     load = pltpu.make_async_copy(vir_hbm, vir, vir_sem)
     load.start()
-    greet([up, down, other] + near[0][0] + near[0][1])
-
-    unit = left_ref.shape[1]
+    greet([up, down, other] + [{"ao": lax.rem(ao + k, groups)} for k in range(1, groups)])
+
+    rows = half_ref.shape[2]
+    mine = pl.ds(pl.multiple_of(ao * rows, 16), rows)
+
+    def piece_copy(s, k):
+        peer = lax.rem(ao + k, groups)
+        return remote(
+            half_ref.at[peer, pl.ds(2 * s, 2)], got.at[pl.ds(2 * s, 2), mine, :],
+            p1_send.at[s, k - 1], p1_recv.at[s, k - 1], {"ao": peer},
+        )
+
+    def slot_of(s):
+        start = pl.multiple_of(ao // 8 * 32 + lax.rem(ao, 2) * 16, 16)
+        return owned.at[s * 4 + lax.rem(ao, 8) // 2, pl.ds(start, 16), :]
+
+    def block_copy(s, k):
+        peer = lax.rem(ao + k, groups)
+        return remote(
+            parts.at[s, peer], slot_of(s), p2_send.at[s, k - 1], p2_recv.at[s, k - 1], {"ao": peer}
+        )
+
+    per_owner = left.shape[2] // 128
+    group_rows = 4 * per_owner * 8
+
+    def sum_blocks(s):
+        both = jnp.concatenate([got[2 * s], got[2 * s + 1]], axis=1)
+
+        def hand(xx):
+            for j in range(4):
+                k = lax.rem(xx * 4 + j - ao + groups, groups)
+
+                @pl.when(k > 0)
+                def _():
+                    block_copy(s, k).start()
+
+        for g in range(4):
+            xx = turn(x, g + 1)
+            pick = pick_ref[pl.ds(pl.multiple_of(xx * group_rows, 16), group_rows), :]
+            total = jnp.dot(pick, both, preferred_element_type=jnp.float32)
+            for j in range(4):
+                for l in range(per_owner):
+                    at = (j * per_owner + l) * 8
+                    tile = jnp.concatenate([total[at:at + 8, :128], total[at:at + 8, 128:]], axis=0)
+                    parts[s, xx * 4 + j, :, 128 * l:128 * l + 128] = tile.astype(jnp.bfloat16)
+            if g > 0:
+                hand(turn(x, g))
+        slot_of(s)[...] = parts[s, ao]
+        hand(x)
+
+    def each_peer(work):
+        def step(k, carry):
+            work(k)
+            return carry
+
+        lax.fori_loop(1, groups, step, 0)
+
+    for s in range(2):
+        each_peer(lambda k: piece_copy(s, k).start())
+    got[:, mine, :] = half_ref[ao]
+    for s in range(2):
+        each_peer(lambda k: piece_copy(s, k).wait_recv())
+        sum_blocks(s)
+
+    unit = owned.shape[1]
     mid = unit // 2
 
     def rows_of(index, start=0, size=unit):
@@ -142,7 +147,7 @@
 
     def own_copy(q, k):
         peer = (up, down, other)[k]
-        return left_copy(q, k, left_ref.at[q], rows_of(aux), peer)
+        return left_copy(q, k, owned.at[q], rows_of(aux), peer)
 
     def half_copy(q, k):
         zz = turn(z, -1) if k == 0 else turn(z, 1)
@@ -157,7 +162,7 @@
     def gather_start(q):
         for k in range(3):
             own_copy(q, k).start()
-        left[q, rows_of(aux)] = left_ref[q]
+        left[q, rows_of(aux)] = owned[q]
 
     def gather_near(q):
         for k in range(2):
@@ -179,12 +184,13 @@
         def tile(n, carry):
             cols = pl.ds(pl.multiple_of(n * 256, 256), 256)
             term = jnp.dot(left[q], vir[:, cols], preferred_element_type=jnp.float32)
-            part[q, :, :, :, :, cols] = term.astype(jnp.bfloat16).reshape(4, 4, 2, 16, 256)
+            part[lax.rem(q, depth), :, :, :, :, cols] = term.astype(jnp.bfloat16).reshape(4, 4, 2, 16, 256)
             return carry
 
         lax.fori_loop(0, vir.shape[1] // 256, tile, 0)
 
     def slab(q, f, a, b):
+        q = lax.rem(q, depth)
         return part.at[q, a, b, 0] if f == 0 else part.at[q, b, a, 1]
 
     half_cols = vir.shape[1] // 2
@@ -254,10 +260,19 @@
             for d in range(2):
                 copy4(q, f, d).wait_recv()
             mine = slab(q, f, major[f], minor[f])
-            out_ref[pl.ds(pl.multiple_of(q * 32 + f * 16, 16), 16), :] = (
+            row = lax.rem(q, 4) * 64 + f * 32 + q // 4 * 16
+            out_ref[pl.ds(pl.multiple_of(row, 16), 16), :] = (
                 wide(mine[...]) + wide(got4[f, 0, q]) + wide(got4[f, 1, q])
             ).astype(jnp.bfloat16)
 
+    def release(q):
+        for f, d in pairs:
+            copy1(q, f, d).wait_send()
+            copy2(q, f, d).wait_send()
+            copy3(q, f, d).wait_send()
+            copy4(q, f, d).wait_send()
+
+    each_peer(lambda k: block_copy(0, k).wait_recv())
     gather_start(0)
     gather_start(1)
     gather_near(0)
@@ -275,6 +290,11 @@
         on(it, gather_wait)
         on(it, multiply)
         on(it, stage1)
+
+        @pl.when(it == 1)
+        def _():
+            each_peer(lambda k: block_copy(1, k).wait_recv())
+
         on(it + 3, gather_start)
         on(it + 2, gather_near)
         on(it - 1, stage2)
@@ -282,9 +302,10 @@
         on(it - 2, stage3)
         on(it - 3, stage4)
         on(it - 4, stage5)
+        on(it - 5, release)
         return carry
 
-    lax.fori_loop(0, chunks + 4, step, 0)
+    lax.fori_loop(0, chunks + 5, step, 0)
 
     def finish(q, carry):
         for k in range(3):
@@ -292,14 +313,12 @@
             side_copy(q, k).wait_send()
         for k in range(2):
             half_copy(q, k).wait_send()
-        for f, d in pairs:
-            copy1(q, f, d).wait_send()
-            copy2(q, f, d).wait_send()
-            copy3(q, f, d).wait_send()
-            copy4(q, f, d).wait_send()
         return carry
 
     lax.fori_loop(0, chunks, finish, 0)
+    for s in range(2):
+        each_peer(lambda k: piece_copy(s, k).wait_send())
+        each_peer(lambda k: block_copy(s, k).wait_send())
 
 
 def params(collective_id, vmem=None):
@@ -355,41 +374,30 @@
     half = jnp.where(in_use[None, :, None, None], half, 0.0).astype(bf16)
     half = half.reshape(groups, depth // groups, slots * occupied, width)
 
-    piece = depth // groups * occupied
-    left = pl.pallas_call(
-        functools.partial(regroup_kernel, groups, per_owner),
-        out_shape=jax.ShapeDtypeStruct((groups, piece, per_owner * width), bf16),
-        in_specs=[spec] * 2,
+    chunks, slots_deep = 8, 6
+    wide = per_owner * width
+    half_sems = [DMA((2, groups - 1))] * 4
+    sems = [DMA((8, chunks)), DMA((8, chunks))] + [DMA((2, 2, chunks))] * 8
+    out = pl.pallas_call(
+        functools.partial(product_kernel, groups, chunks, slots_deep),
+        out_shape=jax.ShapeDtypeStruct((groups * 16, cols), bf16),
+        in_specs=[spec, spec, pl.BlockSpec(memory_space=pl.ANY)],
         out_specs=spec,
         scratch_shapes=[
             VMEM((depth // groups, groups * slots * occupied, width), bf16),
-            VMEM((groups, piece, per_owner * width), bf16),
-            DMA((2, groups - 1)),
-            DMA((2, groups - 1)),
-        ],
-        compiler_params=params(1),
-    )(half, pick)
-
-    chunks = 8
-    left = left.reshape(chunks, 2 * piece, per_owner * width)
-    sems = [DMA((8, chunks)), DMA((8, chunks))] + [DMA((2, 2, chunks))] * 8
-    out = pl.pallas_call(
-        functools.partial(product_kernel, chunks),
-        out_shape=jax.ShapeDtypeStruct((groups * 16, cols), bf16),
-        in_specs=[spec, pl.BlockSpec(memory_space=pl.ANY)],
-        out_specs=spec,
-        scratch_shapes=[
+            VMEM((2, groups, 16, wide), bf16),
+            VMEM((chunks, 64, wide), bf16),
             VMEM(vir_coef.shape, bf16),
-            VMEM((chunks, 8 * 2 * piece, per_owner * width), bf16),
-            VMEM((chunks, 4, 4, 2, 16, cols), bf16),
+            VMEM((chunks, 8 * 64, wide), bf16),
+            VMEM((slots_deep, 4, 4, 2, 16, cols), bf16),
             VMEM((2, 2, chunks, 2, 16, cols), bf16),
             VMEM((2, 2, chunks, 4, 16, cols), bf16),
             VMEM((2, 2, chunks, 16, cols // 2), bf16),
             VMEM((2, 2, chunks, 16, cols), bf16),
             DMA,
-        ] + sems,
-        compiler_params=params(2, 66 * 1024 * 1024 - 3 * 1024 * 1024),
-    )(left, vir_coef)
+        ] + half_sems + sems,
+        compiler_params=params(1, 63 * 1024 * 1024),
+    )(half, pick, vir_coef)
     return out.reshape(-1, occupied, cols)
 
 

time: 201 us -> 190 us (0.945)
  Pallas kernels: 183 us -> 172 us
    pallas_call x2 -> x1, Pallas kernels: 169 us -> 158 us  [per_device(): pl.pallas_call(functools.partial(product_kernel, groups, chunks, slots_de...]
where the time goes in v2:
time: 190 us
  Pallas kernels  172 us (91%)
  local copies, waits for them, and re-layouts  7.67 us (4%)
  matrix products  6.31 us (3%)
  other arithmetic  2.83 us (1%)
    pallas_call x1, Pallas kernels, per_device(): pl.pallas_call(functools.partial(product_kernel, groups, chunks, slots_de...  158 us
    pallas_call x1, Pallas kernels, per_device(): pl.pallas_call(functools.partial(tables_kernel, groups), out_shape=(jax.S...  13.8 us
    dot_general x1, matrix products, per_device(): jnp.einsum('sim,spmn->psin', occ_pick, blocks, preferred_element_type=jnp...  6.31 us

profile of v2, /device:TPU:0, one launch (start us, length us, event | category | flops | bytes accessed | tf_op | source)
XLA Modules:
  0.0 189.6 jit_solution(567231037817586664)
XLA Ops:
  0.7 0.8 slice_bitcast_fusion.1
  1.4 0.7 add_bitcast_fusion
  2.2 0.6 pad.4.ints_ref
  2.8 13.8 %shard_map.64 = (s32[16,8,128]{2,1,0:T(8,128)}, bf16[16,80,128]{2,1,0:T(8,128)(2,1)}) custom-call(s32[8,128]{1,0:T(8,128)} %pad.4.ints_ref, bf16[80,128]{1,0:T(8,128)(2,1)} %bitcast.31), custom_call_target="tpu_custom_call" | custom-call | tf_op jit(solution)/shard_map/pallas_call | solution.py:348
  16.6 0.8 slice.21
  17.4 0.2 slice_reduce_fusion
  17.6 0.1 eq.29
  17.7 0.2 select_reduce_fusion
  17.9 1.5 gather_fusion
  19.5 0.1 multiply_select_fusion
  19.5 0.1 select_n.39
  19.6 0.1 iota_add_fusion.1
  19.7 0.1 add.60
  19.8 0.1 iota_add_fusion
  19.9 0.1 add.56
  20.0 6.3 %fusion = bf16[64,6,8,128]{3,2,0,1:T(8,128)(2,1)S(1)} fusion(bf16[6,64,128,128]{3,2,1,0:T(8,128)(2,1)} %param.6, pred[6]{0:T(512)(128)(4,1)S(1)} %iota_compare_fusion.1, bf16[6,8,128]{2,1,0:T(8,128)(2,1)S(1)} %gather_fusion), kind=kOutput, calls=%fused_computation.3 | convolution fusion | flops 101449728 | bytes 13381638 | tf_op jit(solution)/shard_map/sim,spmn->psin/dot_general | solution.py:372
  26.3 1.0 copy.9
  27.3 1.7 compare_convert_fusion.pick_ref
  29.0 158.2 %shard_map.65 = bf16[256,2304]{1,0:T(8,128)(2,1)} custom-call(bf16[16,4,48,128]{3,2,1,0:T(8,128)(2,1)} %bitcast.27, bf16[1280,768]{1,0:T(8,128)(2,1)} %compare_convert_fusion.pick_ref, bf16[1280,2304]{1,0:T(8,128)(2,1)} %vir_hbm.1), custom_call_target="tpu_custom_call" | custom-call | tf_op jit(solution)/shard_map/pallas_call | solution.py:381
  187.2 2.4 %copy.13 = bf16[32,8,2304]{2,1,0:T(8,128)(2,1)} copy(bf16[32,8,2304]{2,1,0:T(8,128)(2,1)} %bitcast.26) | data formatting | bytes 2359296
  (4 shorter events, 0.0 us)
